TPU v7x, 32 devices: a whole 2x2x4 slice. The times are simulated.
32 devices in a mesh: rep: 8 (over y, x, core), tp: 4 (over z).
Axes of the slice: x: 2, y: 2, z: 4, core: 2. Of those that a mesh axis runs over, the one named last changes fastest.
Arguments:
- flat_buffer: bfloat16 [578912256], P(('rep', 'tp')), may hold values from -60 to 60
- shard_pad: int32 [2, 6], replicated, may hold values from 0 to 2
Outputs:
- q_served: bfloat16 [2, 6144, 6144], P(None, 'rep', 'tp')
- q_scale: float32 [2, 48, 6144], P(None, 'rep', 'tp')
- k_served: bfloat16 [2, 6144, 1024], P(None, 'rep', 'tp')
- k_scale: float32 [2, 48, 1024], P(None, 'rep', 'tp')
- v_served: bfloat16 [2, 6144, 1024], P(None, 'rep', 'tp')
- v_scale: float32 [2, 48, 1024], P(None, 'rep', 'tp')
- o_served: bfloat16 [2, 6144, 6144], P(None, 'tp', 'rep')
- o_scale: float32 [2, 48, 6144], P(None, 'tp', 'rep')
- gate_served: bfloat16 [2, 6144, 16384], P(None, 'rep', 'tp')
- gate_scale: float32 [2, 48, 16384], P(None, 'rep', 'tp')
- up_served: bfloat16 [2, 6144, 16384], P(None, 'rep', 'tp')
- up_scale: float32 [2, 48, 16384], P(None, 'rep', 'tp')
All inputs are finite; a program needn't handle non-finite values. Where the computation divides by a largest or mean magnitude, that divisor is 1e-20 or more.
Results may differ from a plain program's by a relative error of at most 0.001.
Values may be sent and summed in bfloat16 or wider, within the bound.
A program may use at most 192 MiB of HBM per device.

v0:
```python
import jax
import jax.numpy as jnp
from jax import lax
from jax.sharding import PartitionSpec as P

D = 6144
KV = 1024
FF = 16384
GROUP = 128
LAYERS = 2


def quantize(served):
    values = served.astype(jnp.float32)
    grouped = values.reshape(values.shape[0] // GROUP, GROUP, values.shape[1])
    peak = jnp.max(jnp.abs(grouped), axis=1) + 1e-06
    scaled = (grouped / peak[:, None, :]).astype(jnp.bfloat16)
    return (scaled.reshape(served.shape), peak)


def column_block(received):
    return received.reshape(-1, received.shape[3]).T


def output_block(received):
    return received.reshape(-1, received.shape[2]).T


def on_device(flat_buffer, shard_pad):
    devices = lax.axis_size("rep") * lax.axis_size("tp")
    widths = (D, KV, KV, D, FF, FF)
    columns = (0, 1, 2, 4, 5)
    tiled = flat_buffer.reshape(flat_buffer.shape[0] // 128, 128)
    offset = jnp.zeros((), jnp.int32)
    pieces = []
    for layer in range(LAYERS):
        layer_pieces = []
        for index in range(6):
            rows = widths[index] // devices
            lines = rows * D // 128
            taken = lax.dynamic_slice_in_dim(tiled, offset, lines, 0)
            layer_pieces.append(taken.reshape(rows, D))
            offset = offset + lines + shard_pad[layer, index]
        pieces.append(layer_pieces)
    blocks = [[None] * 6 for layer in range(LAYERS)]
    for layer in range(LAYERS):
        for index in columns:
            piece = pieces[layer][index]
            received = lax.all_to_all(
                lax.all_to_all(
                    piece.reshape(1, 1, piece.shape[0], D),
                    "rep",
                    split_axis=3,
                    concat_axis=0,
                    tiled=True,
                ),
                "tp",
                split_axis=0,
                concat_axis=1,
                tiled=True,
            )
            blocks[layer][index] = column_block(received)
        piece = pieces[layer][3]
        received_rows = lax.all_to_all(
            piece.reshape(1, piece.shape[0], D), "tp", split_axis=2, concat_axis=0, tiled=True
        )
        blocks[layer][3] = output_block(received_rows)
    results = []
    for index in range(6):
        scaled_list = []
        peak_list = []
        for layer in range(LAYERS):
            scaled, peak = quantize(blocks[layer][index])
            scaled_list.append(scaled)
            peak_list.append(peak)
        results.append(jnp.stack(scaled_list))
        results.append(jnp.stack(peak_list))
    return (
        results[0],
        results[1],
        results[2],
        results[3],
        results[4],
        results[5],
        results[6],
        results[7],
        results[8],
        results[9],
        results[10],
        results[11],
    )


def solution(mesh):
    return jax.shard_map(
        on_device,
        mesh=mesh,
        in_specs=(P(("rep", "tp")), P()),
        out_specs=(
            P(None, "rep", "tp"),
            P(None, "rep", "tp"),
            P(None, "rep", "tp"),
            P(None, "rep", "tp"),
            P(None, "rep", "tp"),
            P(None, "rep", "tp"),
            P(None, "tp", "rep"),
            P(None, "tp", "rep"),
            P(None, "rep", "tp"),
            P(None, "rep", "tp"),
            P(None, "rep", "tp"),
            P(None, "rep", "tp"),
        ),
        check_vma=False,
    )
```

profile of v0, /device:TPU:10, one launch (start us, length us, event | category | flops | bytes accessed | tf_op | source)
XLA Modules:
  0.0 1923.8 jit_solution(5891359268631695627)
XLA Ops:
  16.2 34.4 %reduce.2 = bf16[6144,32]{1,0:T(8,128)(2,1)} reduce(bf16[6144,1,1,32]{3,2,1,0:T(2,128)(2,1)S(1)} %bitcast.370, bf16[]{:T(256)} %broadcast.224), dimensions={1,2}, to_apply=%bitcast.303.reduce_sub_computation | reduce | bytes 786434
  66.9 34.4 %reduce.3 = bf16[6144,32]{1,0:T(8,128)(2,1)} reduce(bf16[6144,1,1,32]{3,2,1,0:T(2,128)(2,1)S(1)} %bitcast.371, bf16[]{:T(256)} %broadcast.224), dimensions={1,2}, to_apply=%bitcast.301.reduce_sub_computation | reduce | bytes 786434
  117.6 34.4 %reduce.4 = bf16[6144,32]{1,0:T(8,128)(2,1)} reduce(bf16[6144,1,1,32]{3,2,1,0:T(2,128)(2,1)S(1)} %bitcast.372, bf16[]{:T(256)} %broadcast.224), dimensions={1,2}, to_apply=%bitcast.307.reduce_sub_computation | reduce | bytes 786434
  165.6 34.4 %reduce.5 = bf16[6144,32]{1,0:T(8,128)(2,1)} reduce(bf16[6144,1,1,32]{3,2,1,0:T(2,128)(2,1)S(1)} %bitcast.373, bf16[]{:T(256)} %broadcast.224), dimensions={1,2}, to_apply=%bitcast.305.reduce_sub_computation | reduce | bytes 786434
  278.6 13.7 copy.337
  292.3 34.6 %reduce.1 = bf16[6144,192]{1,0:T(8,128)(2,1)S(1)} reduce(bf16[6144,1,1,192]{3,2,1,0:T(2,128)(2,1)} %bitcast.338, bf16[]{:T(256)} %broadcast.224), dimensions={1,2}, to_apply=%bitcast.297.reduce_sub_computation | reduce | bytes 4718594
  341.2 13.7 copy.330
  354.9 34.6 %reduce = bf16[6144,192]{1,0:T(8,128)(2,1)S(1)} reduce(bf16[6144,1,1,192]{3,2,1,0:T(2,128)(2,1)} %bitcast.339, bf16[]{:T(256)} %broadcast.224), dimensions={1,2}, to_apply=%bitcast.299.reduce_sub_computation | reduce | bytes 4718594
  402.0 13.7 copy.372
  415.7 34.6 %reduce.6 = bf16[6144,192]{1,0:T(8,128)(2,1)S(1)} reduce(bf16[6144,1,192]{2,1,0:T(2,128)(2,1)} %bitcast.340, bf16[]{:T(256)} %broadcast.224), dimensions={1}, to_apply=%bitcast.293.reduce_sub_computation | reduce | bytes 4718594
  462.4 13.7 copy.377
  476.1 34.6 %reduce.7 = bf16[6144,192]{1,0:T(8,128)(2,1)S(1)} reduce(bf16[6144,1,192]{2,1,0:T(2,128)(2,1)} %bitcast.341, bf16[]{:T(256)} %broadcast.224), dimensions={1}, to_apply=%bitcast.295.reduce_sub_computation | reduce | bytes 4718594
  522.0 19.1 constant_dynamic-slice_fusion.1
  551.2 26.5 %copy.394 = bf16[1,1,512,6144]{2,1,0,3:T(2,128)(2,1)} copy(bf16[1,1,512,6144]{3,2,1,0:T(8,128)(2,1)} %reshape_reshape.46) | data formatting | bytes 12582912 | tf_op jit(solution)/shard_map/reshape;reshape | solution.py:51
  577.7 41.6 %reduce.10 = bf16[6144,512]{1,0:T(8,128)(2,1)} reduce(bf16[6144,1,1,512]{3,2,1,0:T(2,128)(2,1)} %bitcast.330, bf16[]{:T(256)} %broadcast.224), dimensions={1,2}, to_apply=%bitcast.315.reduce_sub_computation | reduce | bytes 12582914
  645.0 26.5 %copy.400 = bf16[1,1,512,6144]{2,1,0,3:T(2,128)(2,1)} copy(bf16[1,1,512,6144]{3,2,1,0:T(8,128)(2,1)} %reshape_reshape.47) | data formatting | bytes 12582912 | tf_op jit(solution)/shard_map/reshape;reshape | solution.py:51
  671.5 41.7 %reduce.11 = bf16[6144,512]{1,0:T(8,128)(2,1)} reduce(bf16[6144,1,1,512]{3,2,1,0:T(2,128)(2,1)} %bitcast.331, bf16[]{:T(256)} %broadcast.224), dimensions={1,2}, to_apply=%bitcast.313.reduce_sub_computation | reduce | bytes 12582914
  737.7 26.5 %copy.382 = bf16[1,1,512,6144]{2,1,0,3:T(2,128)(2,1)} copy(bf16[1,1,512,6144]{3,2,1,0:T(8,128)(2,1)} %reshape_reshape.44) | data formatting | bytes 12582912 | tf_op jit(solution)/shard_map/reshape;reshape | solution.py:51
  764.2 41.7 %reduce.8 = bf16[6144,512]{1,0:T(8,128)(2,1)} reduce(bf16[6144,1,1,512]{3,2,1,0:T(2,128)(2,1)} %bitcast.332, bf16[]{:T(256)} %broadcast.224), dimensions={1,2}, to_apply=%bitcast.311.reduce_sub_computation | reduce | bytes 12582914
  830.0 26.5 %copy.388 = bf16[1,1,512,6144]{2,1,0,3:T(2,128)(2,1)} copy(bf16[1,1,512,6144]{3,2,1,0:T(8,128)(2,1)} %reshape_reshape.45) | data formatting | bytes 12582912 | tf_op jit(solution)/shard_map/reshape;reshape | solution.py:51
  856.6 41.7 %reduce.9 = bf16[6144,512]{1,0:T(8,128)(2,1)} reduce(bf16[6144,1,1,512]{3,2,1,0:T(2,128)(2,1)} %bitcast.329, bf16[]{:T(256)} %broadcast.224), dimensions={1,2}, to_apply=%bitcast.309.reduce_sub_computation | reduce | bytes 12582914
  920.7 14.0 copy.338
  937.2 45.3 %all-to-all-done.16 = bf16[8,2,196608]{2,1,0:T(2,128)(2,1)} async-done(((bf16[8,2,196608]{2,1,0:T(2,128)(2,1)}), bf16[8,2,196608]{2,1,0:T(2,128)(2,1)}, u32[]{:S(2)}, u32[]{:S(2)}) %all-to-all-start.16) | async-done | bytes 6291488 | tf_op jit(solution)/shard_map/all_to_all | solution.py:50
  996.2 13.3 copy.331
  1013.6 25.0 %all-to-all-done.3 = bf16[8,1,192,768]{3,2,1,0:T(8,128)(2,1)S(1)} async-done(((bf16[8,1,192,768]{3,2,1,0:T(8,128)(2,1)}), bf16[8,1,192,768]{3,2,1,0:T(8,128)(2,1)S(1)}, u32[]{:S(2)}, u32[]{:S(2)}) %all-to-all-start.3) | async-done | bytes 2359328 | tf_op jit(solution)/shard_map/all_to_all | solution.py:49
  1066.5 30.0 %all-to-all-done.1 = bf16[8,1,192,768]{3,2,1,0:T(8,128)(2,1)} async-done(((bf16[8,1,192,768]{3,2,1,0:T(8,128)(2,1)}), bf16[8,1,192,768]{3,2,1,0:T(8,128)(2,1)}, u32[]{:S(2)}, u32[]{:S(2)}) %all-to-all-start.1) | async-done | bytes 2359328 | tf_op jit(solution)/shard_map/all_to_all | solution.py:49
  1125.2 114.3 %all-to-all-done.19 = bf16[8,1,512,768]{2,3,1,0:T(8,128)(2,1)} async-done(((bf16[8,1,512,768]{2,3,1,0:T(8,128)(2,1)}), bf16[8,1,512,768]{2,3,1,0:T(8,128)(2,1)}, u32[]{:S(2)}, u32[]{:S(2)}) %all-to-all-start.19) | async-done | bytes 6291488 | tf_op jit(solution)/shard_map/all_to_all | solution.py:49
  1301.2 13.3 copy.373
  1345.5 13.3 copy.378
  1711.1 16.6 copy.416
  1765.5 12.9 copy.386
  1905.1 16.6 copy.414
  (278 shorter events, 976.0 us)
Async XLA Ops:
  54.4 50.7 %all-to-all-start.4 = ((bf16[8,2,12288]{2,1,0:T(2,128)(2,1)}), bf16[8,2,12288]{2,1,0:T(2,128)(2,1)S(1)}, u32[]{:S(2)}, u32[]{:S(2)}) async-start(bf16[8,2,12288]{2,1,0:T(2,128)(2,1)} %reshape.395), calls=%async_computation.4 | async-start | bytes 786432 | tf_op jit(solution)/shard_map/all_to_all | solution.py:50
  105.1 50.7 %copy-start.12 = (bf16[8,2,12288]{2,1,0:T(2,128)(2,1)}, bf16[8,2,12288]{2,1,0:T(2,128)(2,1)S(1)}, u32[]{:S(2)}) copy-start(bf16[8,2,12288]{2,1,0:T(2,128)(2,1)S(1)} %all-to-all-done.4) | copy-start | bytes 1179652
  105.1 50.7 %all-to-all-start.6 = ((bf16[8,2,12288]{2,1,0:T(2,128)(2,1)}), bf16[8,2,12288]{2,1,0:T(2,128)(2,1)}, u32[]{:S(2)}, u32[]{:S(2)}) async-start(bf16[8,2,12288]{2,1,0:T(2,128)(2,1)} %reshape.393), calls=%async_computation.6 | async-start | bytes 786432 | tf_op jit(solution)/shard_map/all_to_all | solution.py:50
  155.8 48.0 %all-to-all-start.8 = ((bf16[8,2,12288]{2,1,0:T(2,128)(2,1)}), bf16[8,2,12288]{2,1,0:T(2,128)(2,1)}, u32[]{:S(2)}, u32[]{:S(2)}) async-start(bf16[8,2,12288]{2,1,0:T(2,128)(2,1)} %reshape.399), calls=%async_computation.8 | async-start | bytes 786432 | tf_op jit(solution)/shard_map/all_to_all | solution.py:50
  203.8 15.1 all-to-all-start.10
  218.9 16.2 all-to-all-start.5
  235.1 16.2 all-to-all-start.7
  251.3 13.4 all-to-all-start.9
  264.7 67.4 %all-to-all-start.11 = ((bf16[8,1,32,768]{3,2,1,0:T(8,128)(2,1)}), bf16[8,1,32,768]{3,2,1,0:T(8,128)(2,1)S(1)}, u32[]{:S(2)}, u32[]{:S(2)}) async-start(bf16[8,1,32,768]{3,2,1,0:T(8,128)(2,1)} %copy.367), calls=%async_computation.11 | async-start | bytes 786432 | tf_op jit(solution)/shard_map/all_to_all | solution.py:49
  332.1 9.1 copy-start.13
  332.1 62.6 %all-to-all-start.2 = ((bf16[8,2,73728]{2,1,0:T(2,128)(2,1)}), bf16[8,2,73728]{2,1,0:T(2,128)(2,1)}, u32[]{:S(2)}, u32[]{:S(2)}) async-start(bf16[8,2,73728]{2,1,0:T(2,128)(2,1)} %reshape.389), calls=%async_computation.2 | async-start | bytes 4718592 | tf_op jit(solution)/shard_map/all_to_all | solution.py:50
  394.7 60.0 %all-to-all-start = ((bf16[8,2,73728]{2,1,0:T(2,128)(2,1)}), bf16[8,2,73728]{2,1,0:T(2,128)(2,1)}, u32[]{:S(2)}, u32[]{:S(2)}) async-start(bf16[8,2,73728]{2,1,0:T(2,128)(2,1)} %reshape.391), calls=%async_computation | async-start | bytes 4718592 | tf_op jit(solution)/shard_map/all_to_all | solution.py:50
  454.8 60.4 %all-to-all-start.12 = ((bf16[4,2,147456]{2,1,0:T(2,128)(2,1)}), bf16[4,2,147456]{2,1,0:T(2,128)(2,1)}, u32[]{:S(2)}, u32[]{:S(2)}) async-start(bf16[4,2,147456]{2,1,0:T(2,128)(2,1)} %reshape.385), calls=%async_computation.12 | async-start | bytes 4718592 | tf_op jit(solution)/shard_map/all_to_all | solution.py:64
  515.2 113.6 %all-to-all-start.13 = ((bf16[4,2,147456]{2,1,0:T(2,128)(2,1)}), bf16[4,2,147456]{2,1,0:T(2,128)(2,1)S(1)}, u32[]{:S(2)}, u32[]{:S(2)}) async-start(bf16[4,2,147456]{2,1,0:T(2,128)(2,1)} %reshape.387), calls=%async_computation.13 | async-start | bytes 4718592 | tf_op jit(solution)/shard_map/all_to_all | solution.py:64
  630.3 92.3 %all-to-all-start.18 = ((bf16[8,2,196608]{2,1,0:T(2,128)(2,1)}), bf16[8,2,196608]{2,1,0:T(2,128)(2,1)}, u32[]{:S(2)}, u32[]{:S(2)}) async-start(bf16[8,2,196608]{2,1,0:T(2,128)(2,1)} %reshape.407), calls=%async_computation.18 | async-start | bytes 12582912 | tf_op jit(solution)/shard_map/all_to_all | solution.py:50
  722.6 92.7 %all-to-all-start.20 = ((bf16[8,2,196608]{2,1,0:T(2,128)(2,1)}), bf16[8,2,196608]{2,1,0:T(2,128)(2,1)}, u32[]{:S(2)}, u32[]{:S(2)}) async-start(bf16[8,2,196608]{2,1,0:T(2,128)(2,1)} %reshape.405), calls=%async_computation.20 | async-start | bytes 12582912 | tf_op jit(solution)/shard_map/all_to_all | solution.py:50
  815.3 92.3 %all-to-all-start.14 = ((bf16[8,2,196608]{2,1,0:T(2,128)(2,1)}), bf16[8,2,196608]{2,1,0:T(2,128)(2,1)}, u32[]{:S(2)}, u32[]{:S(2)}) async-start(bf16[8,2,196608]{2,1,0:T(2,128)(2,1)} %reshape.403), calls=%async_computation.14 | async-start | bytes 12582912 | tf_op jit(solution)/shard_map/all_to_all | solution.py:50
  907.6 74.9 %all-to-all-start.16 = ((bf16[8,2,196608]{2,1,0:T(2,128)(2,1)}), bf16[8,2,196608]{2,1,0:T(2,128)(2,1)}, u32[]{:S(2)}, u32[]{:S(2)}) async-start(bf16[8,2,196608]{2,1,0:T(2,128)(2,1)} %reshape.401), calls=%async_computation.16 | async-start | bytes 12582912 | tf_op jit(solution)/shard_map/all_to_all | solution.py:50
  982.6 56.1 %all-to-all-start.3 = ((bf16[8,1,192,768]{3,2,1,0:T(8,128)(2,1)}), bf16[8,1,192,768]{3,2,1,0:T(8,128)(2,1)S(1)}, u32[]{:S(2)}, u32[]{:S(2)}) async-start(bf16[8,1,192,768]{3,2,1,0:T(8,128)(2,1)} %copy.339), calls=%async_computation.3 | async-start | bytes 4718592 | tf_op jit(solution)/shard_map/all_to_all | solution.py:49
  1038.6 57.9 %all-to-all-start.1 = ((bf16[8,1,192,768]{3,2,1,0:T(8,128)(2,1)}), bf16[8,1,192,768]{3,2,1,0:T(8,128)(2,1)}, u32[]{:S(2)}, u32[]{:S(2)}) async-start(bf16[8,1,192,768]{3,2,1,0:T(8,128)(2,1)} %copy.332), calls=%async_computation.1 | async-start | bytes 4718592 | tf_op jit(solution)/shard_map/all_to_all | solution.py:49
  1096.5 142.9 %all-to-all-start.19 = ((bf16[8,1,512,768]{2,3,1,0:T(8,128)(2,1)}), bf16[8,1,512,768]{2,3,1,0:T(8,128)(2,1)}, u32[]{:S(2)}, u32[]{:S(2)}) async-start(bf16[8,1,512,768]{2,3,1,0:T(8,128)(2,1)} %bitcast.345), calls=%async_computation.19 | async-start | bytes 12582912 | tf_op jit(solution)/shard_map/all_to_all | solution.py:49
  1239.4 172.2 %all-to-all-start.21 = ((bf16[8,1,512,768]{2,3,1,0:T(8,128)(2,1)}), bf16[8,1,512,768]{2,3,1,0:T(8,128)(2,1)}, u32[]{:S(2)}, u32[]{:S(2)}) async-start(bf16[8,1,512,768]{2,3,1,0:T(8,128)(2,1)} %bitcast.342), calls=%async_computation.21 | async-start | bytes 12582912 | tf_op jit(solution)/shard_map/all_to_all | solution.py:49
  1268.8 8.3 copy-start.14
  1281.4 11.6 copy-start.17
  1411.6 185.0 %all-to-all-start.15 = ((bf16[8,1,512,768]{2,3,1,0:T(8,128)(2,1)}), bf16[8,1,512,768]{2,3,1,0:T(8,128)(2,1)}, u32[]{:S(2)}, u32[]{:S(2)}) async-start(bf16[8,1,512,768]{2,3,1,0:T(8,128)(2,1)} %bitcast.344), calls=%async_computation.15 | async-start | bytes 12582912 | tf_op jit(solution)/shard_map/all_to_all | solution.py:49
  1508.9 11.1 slice-start
  1596.6 187.3 %all-to-all-start.17 = ((bf16[8,1,512,768]{2,3,1,0:T(8,128)(2,1)}), bf16[8,1,512,768]{2,3,1,0:T(8,128)(2,1)}, u32[]{:S(2)}, u32[]{:S(2)}) async-start(bf16[8,1,512,768]{2,3,1,0:T(8,128)(2,1)} %bitcast.343), calls=%async_computation.17 | async-start | bytes 12582912 | tf_op jit(solution)/shard_map/all_to_all | solution.py:49
  1687.9 11.9 copy-start
  1877.1 22.1 %slice-start.2 = ((s8[6291456]{0:T(1024)(128)(4,1)}), s8[2097152]{0:T(1024)(128)(4,1)S(1)}, s32[]{:S(2)}) async-start(s8[6291456]{0:T(1024)(128)(4,1)} %bitcast.354), calls=%async_computation.24 | async-start | bytes 4194304
  1889.8 9.5 slice-start.3
  1905.1 17.5 copy-start.15
  1905.1 17.5 copy-start.16
  (12 other events, 38.1 us)
where the time goes:
time: 1950 us; the launch traced here: 1920 us
  local copies, waits for them, and re-layouts  923 us (47%)
  other arithmetic  653 us (33%)
  waiting for transfers between devices  217 us (11%)
  starting transfers between devices  120 us (6%)
    unnamed x14, other arithmetic  443 us
    unnamed x91, local copies, waits for them, and re-layouts  274 us
    another operation x20, local copies, waits for them, and re-layouts, on_device(): piece.reshape(1, 1, piece.shape[0], D)  204 us
    all_to_all x10, waiting for transfers between devices, on_device(): lax.all_to_all(lax.all_to_all(piece.reshape(1, 1, piece.shape[0], D), 're...  171 us
    div x24, local copies, waits for them, and re-layouts, quantize(): scaled = (grouped / peak[:, None, :]).astype(jnp.bfloat16)  124 us
    abs x12, local copies, waits for them, and re-layouts, quantize(): peak = jnp.max(jnp.abs(grouped), axis=1) + 1e-06  84.2 us
    all_to_all x10, starting transfers between devices, on_device(): lax.all_to_all(lax.all_to_all(piece.reshape(1, 1, piece.shape[0], D), 're...  63.1 us
    convert_element_type x14, local copies, waits for them, and re-layouts, quantize(): values = served.astype(jnp.float32)  61.9 us
  transfers between devices with their start and end apart: 22, of which 5 were waited for; matrix products, arithmetic and copies ran while one was open for 71% of the time, Pallas kernels for 0%

commit v1 on v0

--- a/solution.py
+++ b/solution.py
@@ -46,18 +46,27 @@
     for layer in range(LAYERS):
         for index in columns:
             piece = pieces[layer][index]
-            received = lax.all_to_all(
+            received = jnp.concatenate(
                 lax.all_to_all(
-                    piece.reshape(1, 1, piece.shape[0], D),
-                    "rep",
-                    split_axis=3,
+                    jnp.stack(
+                        jnp.split(
+                            lax.all_to_all(
+                                piece.reshape(1, 1, piece.shape[0], D),
+                                "rep",
+                                split_axis=3,
+                                concat_axis=0,
+                                tiled=True,
+                            ),
+                            lax.psum(1, axis_name="tp"),
+                            0,
+                        ),
+                        0,
+                    ),
+                    axis_name="tp",
+                    split_axis=0,
                     concat_axis=0,
-                    tiled=True,
                 ),
-                "tp",
-                split_axis=0,
-                concat_axis=1,
-                tiled=True,
+                1,
             )
             blocks[layer][index] = column_block(received)
         piece = pieces[layer][3]

time: 1950 us -> 1920 us (0.985)
  local copies, waits for them, and re-layouts: 923 us -> 882 us
  other arithmetic: 653 us -> 673 us
    all_to_all x4 -> x0, local copies, waits for them, and re-layouts: 34.5 us -> none  [on_device(): lax.all_to_all(lax.all_to_all(piece.reshape(1, 1, piece.shape[0], D), 're...]
    another operation x0 -> x10, other arithmetic: none -> 30.3 us  [on_device(): jnp.stack(jnp.split(lax.all_to_all(piece.reshape(1, 1, piece.shape[0], D)...]
    all_to_all x12 -> x6, local copies, waits for them, and re-layouts: 51.5 us -> 44.6 us  [on_device(): lax.all_to_all(piece.reshape(1, 1, piece.shape[0], D), 'rep', split_axis=...]
    unnamed x91 -> x99, local copies, waits for them, and re-layouts: 274 us -> 270 us
    unnamed x14 -> x16, other arithmetic: 443 us -> 443 us
  transfers between devices with their start and end apart: 22 -> 22, of which waited for: 5 -> 6; matrix products, arithmetic and copies ran while one was open for 71% -> 72% of each run, Pallas kernels for 0% -> 0%
where the time goes in v1:
time: 1920 us; the launch traced here: 1890 us
  local copies, waits for them, and re-layouts  882 us (46%)
  other arithmetic  673 us (35%)
  waiting for transfers between devices  208 us (11%)
  starting transfers between devices  120 us (6%)
    unnamed x16, other arithmetic  443 us
    unnamed x99, local copies, waits for them, and re-layouts  270 us
    another operation x20, local copies, waits for them, and re-layouts, on_device(): piece.reshape(1, 1, piece.shape[0], D)  207 us
    all_to_all x10, waiting for transfers between devices, on_device(): lax.all_to_all(jnp.stack(jnp.split(lax.all_to_all(piece.reshape(1, 1, pie...  163 us
    div x24, local copies, waits for them, and re-layouts, quantize(): scaled = (grouped / peak[:, None, :]).astype(jnp.bfloat16)  114 us
    abs x12, local copies, waits for them, and re-layouts, quantize(): peak = jnp.max(jnp.abs(grouped), axis=1) + 1e-06  77.1 us
    convert_element_type x14, local copies, waits for them, and re-layouts, quantize(): values = served.astype(jnp.float32)  69.7 us
    all_to_all x10, starting transfers between devices, on_device(): lax.all_to_all(jnp.stack(jnp.split(lax.all_to_all(piece.reshape(1, 1, pie...  62.6 us
  transfers between devices with their start and end apart: 22, of which 6 were waited for; matrix products, arithmetic and copies ran while one was open for 72% of the time, Pallas kernels for 0%

profile of v1, /device:TPU:10, one launch (start us, length us, event | category | flops | bytes accessed | tf_op | source)
XLA Modules:
  0.0 1892.9 jit_solution(1142161302370312318)
XLA Ops:
  16.2 34.4 %reduce.4 = bf16[6144,32]{1,0:T(8,128)(2,1)} reduce(bf16[6144,1,1,32]{3,2,1,0:T(2,128)(2,1)S(1)} %bitcast.390, bf16[]{:T(256)} %broadcast.224), dimensions={1,2}, to_apply=%bitcast.327.reduce_sub_computation | reduce | bytes 786434
  67.0 34.4 %reduce.5 = bf16[6144,32]{1,0:T(8,128)(2,1)} reduce(bf16[6144,1,1,32]{3,2,1,0:T(2,128)(2,1)S(1)} %bitcast.391, bf16[]{:T(256)} %broadcast.224), dimensions={1,2}, to_apply=%bitcast.325.reduce_sub_computation | reduce | bytes 786434
  118.7 34.4 %reduce.2 = bf16[6144,32]{1,0:T(8,128)(2,1)} reduce(bf16[6144,1,1,32]{3,2,1,0:T(2,128)(2,1)S(1)} %bitcast.392, bf16[]{:T(256)} %broadcast.224), dimensions={1,2}, to_apply=%bitcast.323.reduce_sub_computation | reduce | bytes 786434
  170.1 34.4 %reduce.3 = bf16[6144,32]{1,0:T(8,128)(2,1)} reduce(bf16[6144,1,1,32]{3,2,1,0:T(2,128)(2,1)S(1)} %bitcast.393, bf16[]{:T(256)} %broadcast.224), dimensions={1,2}, to_apply=%bitcast.321.reduce_sub_computation | reduce | bytes 786434
  291.7 13.7 copy.411
  305.4 34.6 %reduce.1 = bf16[6144,192]{1,0:T(8,128)(2,1)S(1)} reduce(bf16[6144,1,1,192]{3,2,1,0:T(2,128)(2,1)} %bitcast.360, bf16[]{:T(256)} %broadcast.224), dimensions={1,2}, to_apply=%bitcast.317.reduce_sub_computation | reduce | bytes 4718594
  354.2 13.7 copy.404
  367.9 34.6 %reduce = bf16[6144,192]{1,0:T(8,128)(2,1)S(1)} reduce(bf16[6144,1,1,192]{3,2,1,0:T(2,128)(2,1)} %bitcast.361, bf16[]{:T(256)} %broadcast.224), dimensions={1,2}, to_apply=%bitcast.319.reduce_sub_computation | reduce | bytes 4718594
  414.6 13.7 copy.446
  428.3 34.6 %reduce.6 = bf16[6144,192]{1,0:T(8,128)(2,1)S(1)} reduce(bf16[6144,1,192]{2,1,0:T(2,128)(2,1)} %bitcast.362, bf16[]{:T(256)} %broadcast.224), dimensions={1}, to_apply=%bitcast.313.reduce_sub_computation | reduce | bytes 4718594
  475.3 13.7 copy.451
  489.0 34.6 %reduce.7 = bf16[6144,192]{1,0:T(8,128)(2,1)S(1)} reduce(bf16[6144,1,192]{2,1,0:T(2,128)(2,1)} %bitcast.363, bf16[]{:T(256)} %broadcast.224), dimensions={1}, to_apply=%bitcast.315.reduce_sub_computation | reduce | bytes 4718594
  534.4 19.1 %constant_dynamic-slice_fusion.1 = (bf16[24576,128]{1,0:T(8,128)(2,1)}, bf16[24576,128]{1,0:T(8,128)(2,1)}, bf16[24576,128]{1,0:T(8,128)(2,1)}, bf16[24576,128]{1,0:T(8,128)(2,1)}) fusion(bf16[141336,128]{1,0:T(8,128)(2,1)} %bitcast.359, s32[]{:T(128)S(6)} %select_n.42, s32[]{:T(128)S(6)} %select_n.43, s32[]{:T(128)S(6)} %select_n.41, s32[]{:T(128)S(6)} %select_n.40), kind=kLoop, calls=%fused_computation.121 | loop fusion | bytes 50331664 | tf_op jit(solution)/shard_map/dynamic_slice | solution.py:41
  563.6 26.5 %copy.468 = bf16[1,1,512,6144]{2,1,0,3:T(2,128)(2,1)} copy(bf16[1,1,512,6144]{3,2,1,0:T(8,128)(2,1)} %reshape_reshape.56) | data formatting | bytes 12582912 | tf_op jit(solution)/shard_map/reshape;reshape | solution.py:54
  590.1 41.6 %reduce.10 = bf16[6144,512]{1,0:T(8,128)(2,1)} reduce(bf16[6144,1,1,512]{3,2,1,0:T(2,128)(2,1)} %bitcast.350, bf16[]{:T(256)} %broadcast.224), dimensions={1,2}, to_apply=%bitcast.335.reduce_sub_computation | reduce | bytes 12582914
  657.7 26.5 %copy.474 = bf16[1,1,512,6144]{2,1,0,3:T(2,128)(2,1)} copy(bf16[1,1,512,6144]{3,2,1,0:T(8,128)(2,1)} %reshape_reshape.57) | data formatting | bytes 12582912 | tf_op jit(solution)/shard_map/reshape;reshape | solution.py:54
  684.3 41.7 %reduce.11 = bf16[6144,512]{1,0:T(8,128)(2,1)} reduce(bf16[6144,1,1,512]{3,2,1,0:T(2,128)(2,1)} %bitcast.351, bf16[]{:T(256)} %broadcast.224), dimensions={1,2}, to_apply=%bitcast.333.reduce_sub_computation | reduce | bytes 12582914
  750.1 26.5 %copy.456 = bf16[1,1,512,6144]{2,1,0,3:T(2,128)(2,1)} copy(bf16[1,1,512,6144]{3,2,1,0:T(8,128)(2,1)} %reshape_reshape.54) | data formatting | bytes 12582912 | tf_op jit(solution)/shard_map/reshape;reshape | solution.py:54
  776.6 41.7 %reduce.8 = bf16[6144,512]{1,0:T(8,128)(2,1)} reduce(bf16[6144,1,1,512]{3,2,1,0:T(2,128)(2,1)} %bitcast.352, bf16[]{:T(256)} %broadcast.224), dimensions={1,2}, to_apply=%bitcast.331.reduce_sub_computation | reduce | bytes 12582914
  843.0 26.5 %copy.462 = bf16[1,1,512,6144]{2,1,0,3:T(2,128)(2,1)} copy(bf16[1,1,512,6144]{3,2,1,0:T(8,128)(2,1)} %reshape_reshape.55) | data formatting | bytes 12582912 | tf_op jit(solution)/shard_map/reshape;reshape | solution.py:54
  869.6 41.7 %reduce.9 = bf16[6144,512]{1,0:T(8,128)(2,1)} reduce(bf16[6144,1,1,512]{3,2,1,0:T(2,128)(2,1)} %bitcast.349, bf16[]{:T(256)} %broadcast.224), dimensions={1,2}, to_apply=%bitcast.329.reduce_sub_computation | reduce | bytes 12582914
  933.7 14.0 copy.412
  955.9 39.6 %all-to-all-done.16 = bf16[8,2,196608]{2,1,0:T(2,128)(2,1)} async-done(((bf16[8,2,196608]{2,1,0:T(2,128)(2,1)}), bf16[8,2,196608]{2,1,0:T(2,128)(2,1)}, u32[]{:S(2)}, u32[]{:S(2)}) %all-to-all-start.16) | async-done | bytes 6291488 | tf_op jit(solution)/shard_map/all_to_all | solution.py:53
  1008.9 13.3 copy.405
  1032.1 19.3 %all-to-all-done.3 = bf16[4,2,1,192,768]{4,1,3,2,0:T(2,128)(2,1)S(1)} async-done(((bf16[4,2,1,192,768]{4,1,3,2,0:T(2,128)(2,1)}), bf16[4,2,1,192,768]{4,1,3,2,0:T(2,128)(2,1)S(1)}, u32[]{:S(2)}, u32[]{:S(2)}) %all-to-all-start.3) | async-done | bytes 2359328 | tf_op jit(solution)/shard_map/all_to_all | solution.py:50
  1080.4 29.1 %all-to-all-done.1 = bf16[4,2,1,192,768]{4,1,3,2,0:T(2,128)(2,1)} async-done(((bf16[4,2,1,192,768]{4,1,3,2,0:T(2,128)(2,1)}), bf16[4,2,1,192,768]{4,1,3,2,0:T(2,128)(2,1)}, u32[]{:S(2)}, u32[]{:S(2)}) %all-to-all-start.1) | async-done | bytes 2359328 | tf_op jit(solution)/shard_map/all_to_all | solution.py:50
  1139.1 113.3 %all-to-all-done.19 = bf16[4,2,1,512,768]{3,4,1,2,0:T(8,128)(2,1)} async-done(((bf16[4,2,1,512,768]{3,4,1,2,0:T(8,128)(2,1)}), bf16[4,2,1,512,768]{3,4,1,2,0:T(8,128)(2,1)}, u32[]{:S(2)}, u32[]{:S(2)}) %all-to-all-start.19) | async-done | bytes 6291488 | tf_op jit(solution)/shard_map/all_to_all | solution.py:50
  1285.9 14.0 copy.447
  1328.2 14.0 copy.452
  1692.0 16.6 copy.490
  1768.4 12.8 copy.465
  1876.1 16.6 copy.488
  (298 shorter events, 957.0 us)
Async XLA Ops:
  54.4 50.8 %all-to-all-start.8 = ((bf16[8,2,12288]{2,1,0:T(2,128)(2,1)}), bf16[8,2,12288]{2,1,0:T(2,128)(2,1)S(1)}, u32[]{:S(2)}, u32[]{:S(2)}) async-start(bf16[8,2,12288]{2,1,0:T(2,128)(2,1)} %reshape.439), calls=%async_computation.8 | async-start | bytes 786432 | tf_op jit(solution)/shard_map/all_to_all | solution.py:53
  105.9 51.0 %all-to-all-start.10 = ((bf16[8,2,12288]{2,1,0:T(2,128)(2,1)}), bf16[8,2,12288]{2,1,0:T(2,128)(2,1)S(1)}, u32[]{:S(2)}, u32[]{:S(2)}) async-start(bf16[8,2,12288]{2,1,0:T(2,128)(2,1)} %reshape.437), calls=%async_computation.10 | async-start | bytes 786432 | tf_op jit(solution)/shard_map/all_to_all | solution.py:53
  157.6 60.7 %all-to-all-start.4 = ((bf16[8,2,12288]{2,1,0:T(2,128)(2,1)}), bf16[8,2,12288]{2,1,0:T(2,128)(2,1)S(1)}, u32[]{:S(2)}, u32[]{:S(2)}) async-start(bf16[8,2,12288]{2,1,0:T(2,128)(2,1)} %reshape.435), calls=%async_computation.4 | async-start | bytes 786432 | tf_op jit(solution)/shard_map/all_to_all | solution.py:53
  219.1 11.0 all-to-all-start.6
  230.2 17.2 all-to-all-start.9
  247.3 17.2 all-to-all-start.11
  264.5 13.5 all-to-all-start.5
  278.0 67.2 %all-to-all-start.7 = ((bf16[4,2,1,32,768]{4,1,3,2,0:T(2,128)(2,1)}), bf16[4,2,1,32,768]{4,1,3,2,0:T(2,128)(2,1)S(1)}, u32[]{:S(2)}, u32[]{:S(2)}) async-start(bf16[4,2,1,32,768]{4,1,3,2,0:T(2,128)(2,1)} %pad_maximum_fusion.13), calls=%async_computation.7 | async-start | bytes 786432 | tf_op jit(solution)/shard_map/all_to_all | solution.py:50
  345.3 6.5 copy-start.16
  345.3 62.4 %all-to-all-start.2 = ((bf16[8,2,73728]{2,1,0:T(2,128)(2,1)}), bf16[8,2,73728]{2,1,0:T(2,128)(2,1)}, u32[]{:S(2)}, u32[]{:S(2)}) async-start(bf16[8,2,73728]{2,1,0:T(2,128)(2,1)} %reshape.429), calls=%async_computation.2 | async-start | bytes 4718592 | tf_op jit(solution)/shard_map/all_to_all | solution.py:53
  407.7 59.7 %all-to-all-start = ((bf16[8,2,73728]{2,1,0:T(2,128)(2,1)}), bf16[8,2,73728]{2,1,0:T(2,128)(2,1)}, u32[]{:S(2)}, u32[]{:S(2)}) async-start(bf16[8,2,73728]{2,1,0:T(2,128)(2,1)} %reshape.431), calls=%async_computation | async-start | bytes 4718592 | tf_op jit(solution)/shard_map/all_to_all | solution.py:53
  467.4 60.7 %all-to-all-start.12 = ((bf16[4,2,147456]{2,1,0:T(2,128)(2,1)}), bf16[4,2,147456]{2,1,0:T(2,128)(2,1)}, u32[]{:S(2)}, u32[]{:S(2)}) async-start(bf16[4,2,147456]{2,1,0:T(2,128)(2,1)} %reshape.425), calls=%async_computation.12 | async-start | bytes 4718592 | tf_op jit(solution)/shard_map/all_to_all | solution.py:73
  528.1 113.2 %all-to-all-start.13 = ((bf16[4,2,147456]{2,1,0:T(2,128)(2,1)}), bf16[4,2,147456]{2,1,0:T(2,128)(2,1)S(1)}, u32[]{:S(2)}, u32[]{:S(2)}) async-start(bf16[4,2,147456]{2,1,0:T(2,128)(2,1)} %reshape.427), calls=%async_computation.13 | async-start | bytes 4718592 | tf_op jit(solution)/shard_map/all_to_all | solution.py:73
  642.7 92.6 %all-to-all-start.18 = ((bf16[8,2,196608]{2,1,0:T(2,128)(2,1)}), bf16[8,2,196608]{2,1,0:T(2,128)(2,1)}, u32[]{:S(2)}, u32[]{:S(2)}) async-start(bf16[8,2,196608]{2,1,0:T(2,128)(2,1)} %reshape.447), calls=%async_computation.18 | async-start | bytes 12582912 | tf_op jit(solution)/shard_map/all_to_all | solution.py:53
  735.3 92.5 %all-to-all-start.20 = ((bf16[8,2,196608]{2,1,0:T(2,128)(2,1)}), bf16[8,2,196608]{2,1,0:T(2,128)(2,1)}, u32[]{:S(2)}, u32[]{:S(2)}) async-start(bf16[8,2,196608]{2,1,0:T(2,128)(2,1)} %reshape.445), calls=%async_computation.20 | async-start | bytes 12582912 | tf_op jit(solution)/shard_map/all_to_all | solution.py:53
  827.8 92.9 %all-to-all-start.14 = ((bf16[8,2,196608]{2,1,0:T(2,128)(2,1)}), bf16[8,2,196608]{2,1,0:T(2,128)(2,1)}, u32[]{:S(2)}, u32[]{:S(2)}) async-start(bf16[8,2,196608]{2,1,0:T(2,128)(2,1)} %reshape.443), calls=%async_computation.14 | async-start | bytes 12582912 | tf_op jit(solution)/shard_map/all_to_all | solution.py:53
  920.7 74.9 %all-to-all-start.16 = ((bf16[8,2,196608]{2,1,0:T(2,128)(2,1)}), bf16[8,2,196608]{2,1,0:T(2,128)(2,1)}, u32[]{:S(2)}, u32[]{:S(2)}) async-start(bf16[8,2,196608]{2,1,0:T(2,128)(2,1)} %reshape.441), calls=%async_computation.16 | async-start | bytes 12582912 | tf_op jit(solution)/shard_map/all_to_all | solution.py:53
  995.6 55.9 %all-to-all-start.3 = ((bf16[4,2,1,192,768]{4,1,3,2,0:T(2,128)(2,1)}), bf16[4,2,1,192,768]{4,1,3,2,0:T(2,128)(2,1)S(1)}, u32[]{:S(2)}, u32[]{:S(2)}) async-start(bf16[4,2,1,192,768]{4,1,3,2,0:T(2,128)(2,1)} %pad_maximum_fusion.9), calls=%async_computation.3 | async-start | bytes 4718592 | tf_op jit(solution)/shard_map/all_to_all | solution.py:50
  1051.4 18.9 copy-start.7
  1051.4 58.0 %all-to-all-start.1 = ((bf16[4,2,1,192,768]{4,1,3,2,0:T(2,128)(2,1)}), bf16[4,2,1,192,768]{4,1,3,2,0:T(2,128)(2,1)}, u32[]{:S(2)}, u32[]{:S(2)}) async-start(bf16[4,2,1,192,768]{4,1,3,2,0:T(2,128)(2,1)} %pad_maximum_fusion.8), calls=%async_computation.1 | async-start | bytes 4718592 | tf_op jit(solution)/shard_map/all_to_all | solution.py:50
  1109.4 143.0 %all-to-all-start.19 = ((bf16[4,2,1,512,768]{3,4,1,2,0:T(8,128)(2,1)}), bf16[4,2,1,512,768]{3,4,1,2,0:T(8,128)(2,1)}, u32[]{:S(2)}, u32[]{:S(2)}) async-start(bf16[4,2,1,512,768]{3,4,1,2,0:T(8,128)(2,1)} %pad_maximum_fusion.4), calls=%async_computation.19 | async-start | bytes 12582912 | tf_op jit(solution)/shard_map/all_to_all | solution.py:50
  1252.4 191.4 %all-to-all-start.21 = ((bf16[4,2,1,512,768]{3,4,1,2,0:T(8,128)(2,1)}), bf16[4,2,1,512,768]{3,4,1,2,0:T(8,128)(2,1)}, u32[]{:S(2)}, u32[]{:S(2)}) async-start(bf16[4,2,1,512,768]{3,4,1,2,0:T(8,128)(2,1)} %pad_maximum_fusion.5), calls=%async_computation.21 | async-start | bytes 12582912 | tf_op jit(solution)/shard_map/all_to_all | solution.py:50
  1376.3 10.9 slice-start.2
  1382.4 6.4 copy-start.5
  1419.7 20.5 %slice-start.4 = ((s8[6291456]{0:T(1024)(128)(4,1)}), s8[2097152]{0:T(1024)(128)(4,1)S(1)}, s32[]{:S(2)}) async-start(s8[6291456]{0:T(1024)(128)(4,1)} %bitcast.365), calls=%async_computation.26 | async-start | bytes 4194304
  1431.0 9.3 slice-start.5
  1443.8 152.3 %all-to-all-start.15 = ((bf16[4,2,1,512,768]{3,4,1,2,0:T(8,128)(2,1)}), bf16[4,2,1,512,768]{3,4,1,2,0:T(8,128)(2,1)}, u32[]{:S(2)}, u32[]{:S(2)}) async-start(bf16[4,2,1,512,768]{3,4,1,2,0:T(8,128)(2,1)} %pad_maximum_fusion.2), calls=%async_computation.15 | async-start | bytes 12582912 | tf_op jit(solution)/shard_map/all_to_all | solution.py:50
  1500.8 10.7 slice-start
  1596.1 162.9 %all-to-all-start.17 = ((bf16[4,2,1,512,768]{3,4,1,2,0:T(8,128)(2,1)}), bf16[4,2,1,512,768]{3,4,1,2,0:T(8,128)(2,1)}, u32[]{:S(2)}, u32[]{:S(2)}) async-start(bf16[4,2,1,512,768]{3,4,1,2,0:T(8,128)(2,1)} %pad_maximum_fusion.3), calls=%async_computation.17 | async-start | bytes 12582912 | tf_op jit(solution)/shard_map/all_to_all | solution.py:50
  1668.7 11.9 copy-start
  1848.0 22.1 %slice-start.6 = ((s8[6291456]{0:T(1024)(128)(4,1)}), s8[2097152]{0:T(1024)(128)(4,1)S(1)}, s32[]{:S(2)}) async-start(s8[6291456]{0:T(1024)(128)(4,1)} %bitcast.374), calls=%async_computation.28 | async-start | bytes 4194304
  1860.8 9.5 slice-start.7
  (16 other events, 48.5 us)
